TPU v7x, 32 devices: a whole 2x2x4 slice. The times are simulated.
32 devices in a mesh: dp: 8 (over y, x, core), tensor: 4 (over z).
Axes of the slice: x: 2, y: 2, z: 4, core: 2. Of those that a mesh axis runs over, the one named last changes fastest.
Arguments:
- teacher_in: bfloat16 [2048, 2048], P('dp'), may hold values from -13 to 13
- teacher_gain: float32 [2, 2048], replicated, may hold values from 0.25 to 1.75
- t_gate: bfloat16 [2, 2048, 5472], P(None, 'dp', 'tensor'), may hold values from -0.125 to 0.125
- t_up: bfloat16 [2, 2048, 5472], P(None, 'dp', 'tensor'), may hold values from -0.125 to 0.125
- t_down: bfloat16 [2, 5472, 2048], P(None, 'tensor', 'dp'), may hold values from -0.078125 to 0.078125
- student_in: bfloat16 [2048, 1024], P('dp'), may hold values from -13 to 13
- student_gain: float32 [2, 1024], replicated, may hold values from 0.3 to 3.5
- s_gate: bfloat16 [2, 1024, 4096], P(None, None, 'tensor'), may hold values from -0.1875 to 0.1875
- s_up: bfloat16 [2, 1024, 4096], P(None, None, 'tensor'), may hold values from -0.1875 to 0.1875
- s_down: bfloat16 [2, 4096, 1024], P(None, 'tensor'), may hold values from -0.09375 to 0.09375
- proj: bfloat16 [1024, 2048], P(None, 'tensor'), may hold values from -1 to 1
- layer_map: int32 [2], replicated, may hold values from 0 to 1, each once
Outputs:
- teacher_states: bfloat16 [2, 2048, 2048], P(None, ('dp', 'tensor'))
- grad_gate: float32 [2, 1024, 4096], P(None, 'dp', 'tensor')
- grad_up: float32 [2, 1024, 4096], P(None, 'dp', 'tensor')
- grad_down: float32 [2, 4096, 1024], P(None, 'tensor', 'dp')
- grad_proj: float32 [1024, 2048], P('dp', 'tensor')
- mean_error: float32 [2], replicated
- grad_rms: float32 [4], replicated
Inputs may be any that keep to these rules, and one draw needn't show every extreme that they name: `layer_map`: each teacher sublayer is matched to exactly one student sublayer.
All inputs are finite; a program needn't handle non-finite values.
Results may differ from a plain program's by a relative error of at most 0.02.
Values may be sent and summed in bfloat16 or wider, within the bound.
No kernel may reach another device: no remote copies, remote signals or barrier semaphores. Data moves between devices by JAX's collectives and lax.ppermute only.
A program may use at most 128 MiB of HBM per device.

v0:
```python
import jax
import jax.numpy as jnp
from jax import lax
from jax.sharding import PartitionSpec as P

DT = 2048
DS = 1024
FS = 4096
T_LAYERS = 2
S_LAYERS = 2
SEQ = 512
EPSILON = 1e-05


def inverse_rms(values):
    return lax.rsqrt(jnp.mean(values * values, axis=-1, keepdims=True) + EPSILON)


def contract_rows(left, right):
    return lax.dot_general(
        left, right, (((0,), (0,)), ((), ())), preferred_element_type=jnp.float32
    )


def contract_cols(left, right):
    return lax.dot_general(
        left, right, (((1,), (1,)), ((), ())), preferred_element_type=jnp.float32
    )


def per_device(
    teacher_in,
    teacher_gain,
    t_gate,
    t_up,
    t_down,
    student_in,
    student_gain,
    s_gate,
    s_up,
    s_down,
    proj,
    layer_map,
):
    tensor_count = lax.axis_size("tensor")
    tensor_pos = lax.axis_index("tensor")
    token_count = teacher_in.shape[0]
    own_rows = token_count // tensor_count
    row_start = tensor_pos * own_rows
    state = teacher_in
    own_states = []
    full_states = []
    for k in range(T_LAYERS):
        state_wide = state.astype(jnp.float32)
        normed = (state_wide * inverse_rms(state_wide) * teacher_gain[k]).astype(jnp.bfloat16)
        gate_act = jnp.dot(
            normed,
            lax.all_gather(t_gate[k], "dp", axis=0, tiled=True),
            preferred_element_type=jnp.float32,
        )
        up_act = jnp.dot(
            normed,
            lax.all_gather(t_up[k], "dp", axis=0, tiled=True),
            preferred_element_type=jnp.float32,
        )
        hidden = (jax.nn.silu(gate_act) * up_act).astype(jnp.bfloat16)
        down_full = lax.all_gather(t_down[k], "dp", axis=1, tiled=True)
        summed = lax.psum(
            jnp.dot(hidden, down_full, preferred_element_type=jnp.float32).astype(jnp.bfloat16),
            "tensor",
        ).astype(jnp.float32)
        state = (state_wide + summed).astype(jnp.bfloat16)
        own_new = lax.dynamic_slice_in_dim(state, row_start, own_rows, 0)
        own_states.append(own_new)
        full_states.append(state)
    col_width = proj.shape[1]
    col_start = tensor_pos * col_width
    targets = jnp.stack(
        [lax.dynamic_slice_in_dim(full, col_start, col_width, 1) for full in full_states]
    )
    states = [student_in]
    normeds, gates, ups, units, scales = ([], [], [], [], [])
    for l in range(S_LAYERS):
        wide = states[l].astype(jnp.float32)
        scale = inverse_rms(wide)
        normed = (wide * scale * student_gain[l]).astype(jnp.bfloat16)
        gate_act = jnp.dot(normed, s_gate[l], preferred_element_type=jnp.float32)
        up_act = jnp.dot(normed, s_up[l], preferred_element_type=jnp.float32)
        units_now = (jax.nn.silu(gate_act) * up_act).astype(jnp.bfloat16)
        down_now = s_down[l]
        student_part = lax.psum_scatter(
            jnp.dot(units_now, down_now, preferred_element_type=jnp.float32).astype(jnp.bfloat16),
            "tensor",
            scatter_dimension=0,
            tiled=True,
        ).astype(jnp.float32)
        own_wide = lax.dynamic_slice_in_dim(wide, row_start, own_rows, 0)
        own_next = (own_wide + student_part).astype(jnp.bfloat16)
        states.append(lax.all_gather(own_next, "tensor", axis=0, tiled=True))
        normeds.append(normed)
        gates.append(gate_act)
        ups.append(up_act)
        units.append(units_now)
        scales.append(scale)
    error_parts = []
    deltas = []
    for l in range(S_LAYERS):
        predicted = jnp.dot(states[l + 1], proj, preferred_element_type=jnp.float32)
        target = lax.dynamic_index_in_dim(targets, layer_map[l], 0, keepdims=False).astype(
            jnp.float32
        )
        errors = predicted - target
        error_parts.append(jnp.sum(errors * errors))
        deltas.append((errors * (2.0 / (S_LAYERS * SEQ))).astype(jnp.bfloat16))
    error_local = jnp.stack(error_parts)
    error_total = lax.psum(error_local, ("dp", "tensor"))
    grad_x = lax.psum(
        contract_cols(deltas[S_LAYERS - 1], proj).astype(jnp.bfloat16), "tensor"
    ).astype(jnp.float32)
    gate_grads = [None] * S_LAYERS
    up_grads = [None] * S_LAYERS
    down_grads = [None] * S_LAYERS
    for l in reversed(range(S_LAYERS)):
        grad_out = grad_x.astype(jnp.bfloat16)
        grad_units = contract_cols(grad_out, s_down[l])
        sigma = jax.nn.sigmoid(gates[l])
        grad_gate_act = (grad_units * ups[l] * sigma * (1.0 + gates[l] * (1.0 - sigma))).astype(
            jnp.bfloat16
        )
        grad_up_act = (grad_units * jax.nn.silu(gates[l])).astype(jnp.bfloat16)
        gate_grads[l] = contract_rows(normeds[l], grad_gate_act)
        up_grads[l] = contract_rows(normeds[l], grad_up_act)
        down_grads[l] = contract_rows(units[l], grad_out)
        if l > 0:
            norm_part = contract_cols(grad_gate_act, s_gate[l]) + contract_cols(
                grad_up_act, s_up[l]
            )
            proj_part = contract_cols(deltas[l - 1], proj)
            grad_norm, grad_side = (
                lax.psum(norm_part.astype(jnp.bfloat16), "tensor").astype(jnp.float32),
                lax.psum(proj_part.astype(jnp.bfloat16), "tensor").astype(jnp.float32),
            )
            wide = states[l].astype(jnp.float32)
            scaled = grad_norm * student_gain[l]
            through = scales[l] * scaled - wide * scales[l] ** 3 * jnp.mean(
                wide * scaled, axis=-1, keepdims=True
            )
            grad_x = grad_x + through + grad_side
    proj_local = contract_rows(states[1], deltas[0])
    l = 1
    proj_local = proj_local + contract_rows(states[l + 1], deltas[l])
    grad_gate, grad_up, grad_down, grad_proj = (
        lax.psum_scatter(
            jnp.stack(gate_grads).astype(jnp.bfloat16), "dp", scatter_dimension=1, tiled=True
        ).astype(jnp.float32),
        lax.psum_scatter(
            jnp.stack(up_grads).astype(jnp.bfloat16), "dp", scatter_dimension=1, tiled=True
        ).astype(jnp.float32),
        lax.psum_scatter(
            jnp.stack(down_grads).astype(jnp.bfloat16), "dp", scatter_dimension=2, tiled=True
        ).astype(jnp.float32),
        lax.psum_scatter(
            proj_local.astype(jnp.bfloat16), "dp", scatter_dimension=0, tiled=True
        ).astype(jnp.float32),
    )
    squares = jnp.stack(
        [
            jnp.sum(grad_gate * grad_gate),
            jnp.sum(grad_up * grad_up),
            jnp.sum(grad_down * grad_down),
            jnp.sum(grad_proj * grad_proj),
        ]
    )
    square_total = lax.psum(squares, ("dp", "tensor"))
    counts = jnp.array(
        [S_LAYERS * DS * FS, S_LAYERS * DS * FS, S_LAYERS * DS * FS, DS * DT], jnp.float32
    )
    mean_error = error_total / (token_count * lax.axis_size("dp") * DT)
    grad_rms = jnp.sqrt(square_total / counts)
    return (jnp.stack(own_states), grad_gate, grad_up, grad_down, grad_proj, mean_error, grad_rms)


def solution(mesh):
    return jax.shard_map(
        per_device,
        mesh=mesh,
        in_specs=(
            P("dp", None),
            P(),
            P(None, "dp", "tensor"),
            P(None, "dp", "tensor"),
            P(None, "tensor", "dp"),
            P("dp", None),
            P(),
            P(None, None, "tensor"),
            P(None, None, "tensor"),
            P(None, "tensor", None),
            P(None, "tensor"),
            P(),
        ),
        out_specs=(
            P(None, ("dp", "tensor"), None),
            P(None, "dp", "tensor"),
            P(None, "dp", "tensor"),
            P(None, "tensor", "dp"),
            P("dp", "tensor"),
            P(),
            P(),
        ),
        check_vma=False,
    )
```

profile of v0, /device:TPU:0, one launch (start us, length us, event | category | flops | bytes accessed | tf_op | source)
XLA Modules:
  0.0 709.6 jit_solution(3058975793029169596)
XLA Ops:
  8.1 2.7 fusion.110
  12.1 2.5 fusion.112
  14.9 2.5 fusion.56
  23.0 34.2 %all-gather.13.cloned.1.call-done = bf16[1,2048,1368]{1,2,0:T(8,128)(2,1)} async-done(((bf16[1,256,1368]{1,2,0:T(8,128)(2,1)}), bf16[1,2048,1368]{1,2,0:T(8,128)(2,1)}) %all-gather.13.cloned.1.call-update) | async-done | bytes 5603344 | tf_op jit(solution)/shard_map/all_gather | solution.py:58
  57.2 5.5 fusion.10
  62.6 40.5 %all-gather.15.cloned.1.call-done = bf16[1,2048,1368]{1,2,0:T(8,128)(2,1)} async-done(((bf16[1,256,1368]{1,2,0:T(8,128)(2,1)}), bf16[1,2048,1368]{1,2,0:T(8,128)(2,1)}) %all-gather.15.cloned.1.call-update) | async-done | bytes 5603344 | tf_op jit(solution)/shard_map/all_gather | solution.py:63
  103.2 46.0 %all-gather.17.cloned.1.call-done = bf16[1,1368,2048]{2,1,0:T(8,128)(2,1)} async-done(((bf16[1,1368,256]{2,1,0:T(8,128)(2,1)}), bf16[1,1368,2048]{2,1,0:T(8,128)(2,1)}) %all-gather.17.cloned.1.call-update) | async-done | bytes 5603344 | tf_op jit(solution)/shard_map/all_gather | solution.py:67
  149.2 11.8 %fusion.24 = bf16[256,2048]{1,0:T(8,128)(2,1)} fusion(bf16[1,1368,2048]{2,1,0:T(8,128)(2,1)} %all-gather.17.cloned.1.call-done, bf16[1,2048,1368]{1,2,0:T(8,128)(2,1)} %all-gather.15.cloned.1.call-done, f32[256,1368]{0,1:T(8,128)} %fusion.10, bf16[256,2048]{1,0:T(8,128)(2,1)S(1)} %copy-done.3, f32[2048]{0:T(1024)S(1)} %bitcast.152, f32[256]{0:T(256)S(1)} %add_rsqrt_fusion.3), kind=kOutput, calls=%fused_computation.25 | convolution fusion | flops 2873626624 | bytes 14713856 | tf_op jit(solution)/shard_map/dot_general | solution.py:69
  164.0 23.2 %all_gather.30 = bf16[256,1024]{1,0:T(8,128)(2,1)S(1)} all-gather(bf16[64,1024]{1,0:T(8,128)(2,1)S(1)} %add_convert_fusion.3), channel_id=1, replica_groups=mesh['dp'=8,'tensor'=4] {'tensor'}, dimensions={0}, use_global_device_ids=true | all-gather | bytes 655360 | tf_op jit(solution)/shard_map/all_gather | solution.py:99
  187.4 2.6 fusion.48
  195.3 25.4 %all-reduce.7.cloned.1.call-done = bf16[256,2048]{1,0:T(8,128)(2,1)} async-done(((bf16[256,2048]{1,0:T(8,128)(2,1)}), bf16[256,2048]{1,0:T(8,128)(2,1)}) %all-reduce.7.cloned.1.call-update) | async-done | bytes 1048592 | tf_op jit(solution)/shard_map/psum | solution.py:68
  222.8 5.5 fusion.4
  228.2 24.1 %all-gather.21.cloned.1.call-done = bf16[1,2048,1368]{1,2,0:T(8,128)(2,1)} async-done(((bf16[1,256,1368]{1,2,0:T(8,128)(2,1)}), bf16[1,2048,1368]{1,2,0:T(8,128)(2,1)}) %all-gather.21.cloned.1.call-update) | async-done | bytes 5603344 | tf_op jit(solution)/shard_map/all_gather | solution.py:63
  252.3 45.3 %all-gather.23.cloned.1.call-done = bf16[1,1368,2048]{2,1,0:T(8,128)(2,1)} async-done(((bf16[1,1368,256]{2,1,0:T(8,128)(2,1)}), bf16[1,1368,2048]{2,1,0:T(8,128)(2,1)}) %all-gather.23.cloned.1.call-update) | async-done | bytes 5603344 | tf_op jit(solution)/shard_map/all_gather | solution.py:67
  297.6 11.8 %fusion.27 = bf16[256,2048]{1,0:T(8,128)(2,1)} fusion(bf16[1,1368,2048]{2,1,0:T(8,128)(2,1)} %all-gather.23.cloned.1.call-done, bf16[1,2048,1368]{1,2,0:T(8,128)(2,1)} %all-gather.21.cloned.1.call-done, f32[256,1368]{0,1:T(8,128)} %fusion.4, bf16[256,2048]{1,0:T(8,128)(2,1)S(1)} %get-tuple-element.20, f32[2048]{0:T(1024)S(1)} %bitcast.150, ...), kind=kOutput, calls=%fused_computation.26 | convolution fusion | flops 2873626624 | bytes 14713856 | tf_op jit(solution)/shard_map/dot_general | solution.py:69
  316.2 22.9 %all_gather.31 = bf16[256,1024]{1,0:T(8,128)(2,1)} all-gather(bf16[64,1024]{1,0:T(8,128)(2,1)S(1)} %add_convert_fusion.2), channel_id=1, replica_groups=mesh['dp'=8,'tensor'=4] {'tensor'}, dimensions={0}, use_global_device_ids=true | all-gather | bytes 655360 | tf_op jit(solution)/shard_map/all_gather | solution.py:99
  339.1 30.7 %all-reduce.9.cloned.1.call-done = bf16[256,2048]{1,0:T(8,128)(2,1)} async-done(((bf16[256,2048]{1,0:T(8,128)(2,1)}), bf16[256,2048]{1,0:T(8,128)(2,1)}) %all-reduce.9.cloned.1.call-update) | async-done | bytes 1048592 | tf_op jit(solution)/shard_map/psum | solution.py:68
  380.1 33.7 %all-reduce.11.cloned.1.call-done = bf16[256,1024]{1,0:T(8,128)(2,1)} async-done(((bf16[256,1024]{1,0:T(8,128)(2,1)}), bf16[256,1024]{1,0:T(8,128)(2,1)}) %all-reduce.11.cloned.1.call-update) | async-done | bytes 524304 | tf_op jit(solution)/shard_map/psum | solution.py:117
  413.8 3.5 multiply_convert_fusion.2
  423.3 3.1 convert_bitcast_fusion
  426.5 45.5 %all-reduce.13.cloned.1.call-done = (bf16[256,1024]{1,0:T(8,128)(2,1)}, bf16[256,1024]{1,0:T(8,128)(2,1)}) async-done(((bf16[256,1024]{1,0:T(8,128)(2,1)}, bf16[256,1024]{1,0:T(8,128)(2,1)}), (bf16[256,1024]{1,0:T(8,128)(2,1)}, bf16[256,1024]{1,0:T(8,128)(2,1)})) %all-reduce.13.cloned.1.call-update) | async-done | bytes 1048592 | tf_op jit(solution)/shard_map/psum | solution.py:141
  476.6 2.3 pad_maximum_fusion.2
  478.9 11.3 %copy.20 = bf16[2,1024,1024]{1,0,2:T(2,128)(2,1)} copy(bf16[2,1024,1024]{2,1,0:T(8,128)(2,1)} %pad_maximum_fusion.2) | data formatting | bytes 8388608
  490.2 5.6 copy.22
  497.7 2.4 fusion.50
  515.6 30.8 %reduce-scatter.19.cloned.1.call-done = bf16[128,2048]{1,0:T(8,128)(2,1)} async-done(((bf16[1024,2048]{1,0:T(8,128)(2,1)}), bf16[128,2048]{1,0:T(8,128)(2,1)}) %reduce-scatter.19.cloned.1.call-update) | async-done | bytes 524304
  550.2 50.8 %reduce-scatter.15.cloned.1.call-done = bf16[2,128,1024]{2,1,0:T(8,128)(2,1)} async-done(((bf16[2,1024,1024]{2,1,0:T(8,128)(2,1)}), bf16[2,128,1024]{2,1,0:T(8,128)(2,1)}) %reduce-scatter.15.cloned.1.call-update) | async-done | bytes 524304 | tf_op jit(solution)/shard_map/reduce_scatter | solution.py:156
  601.0 2.8 multiply_reduce_fusion.1
  603.8 51.5 %reduce-scatter.13.cloned.1.call-done = bf16[2,128,1024]{2,1,0:T(8,128)(2,1)} async-done(((bf16[2,1024,1024]{2,1,0:T(8,128)(2,1)}), bf16[2,128,1024]{2,1,0:T(8,128)(2,1)}) %reduce-scatter.13.cloned.1.call-update) | async-done | bytes 524304 | tf_op jit(solution)/shard_map/reduce_scatter | solution.py:153
  655.3 2.8 multiply_reduce_fusion.2
  658.1 2.6 pad_maximum_fusion.5
  661.6 39.2 %all-reduce = (f32[2]{0:T(128)S(1)}, f32[4]{0:T(128)S(1)}) all-reduce(f32[2]{0:T(128)S(1)} %pad_maximum_fusion.4, f32[4]{0:T(128)S(1)} %pad_maximum_fusion.5), channel_id=1, replica_groups=mesh['dp'=8,'tensor'=4] {'dp','tensor'}, use_global_device_ids=true, to_apply=%region_18.19 | all-reduce | flops 6 | bytes 48 | tf_op jit(solution)/shard_map/psum | solution.py:116
  (165 shorter events, 63.9 us)
Async XLA Ops:
  8.0 364.4 %copy-start = (bf16[1024,512]{1,0:T(8,128)(2,1)S(1)}, bf16[1024,512]{1,0:T(8,128)(2,1)}, u32[]{:S(2)}) copy-start(bf16[1024,512]{1,0:T(8,128)(2,1)} %param.23) | copy-start | bytes 3145732
  8.0 2.8 copy-start.13
  8.0 49.1 %all-gather.13.cloned.1.call-start = ((), (), s32[]{:S(2)}) async-start(), calls=%async_computation.14 | async-start | bytes 6303744 | tf_op jit(solution)/shard_map/all_gather | solution.py:58
  10.7 92.4 %all-gather.15.cloned.1.call-start = ((), (), s32[]{:S(2)}) async-start(), calls=%async_computation.15 | async-start | bytes 6303744 | tf_op jit(solution)/shard_map/all_gather | solution.py:63
  12.0 2.7 copy-start.5
  12.0 2.9 copy-start.23
  12.0 137.2 %all-gather.17.cloned.1.call-start = ((), (), s32[]{:S(2)}) async-start(), calls=%async_computation.16 | async-start | bytes 6303744 | tf_op jit(solution)/shard_map/all_gather | solution.py:67
  14.6 148.4 %reduce-scatter.9.cloned.1.call-start = ((), (), s32[]{:S(2)}) async-start(), calls=%async_computation.8 | async-start | bytes 655360 | tf_op jit(solution)/shard_map/reduce_scatter | solution.py:91
  14.9 2.8 copy-start.25
  17.7 3.3 copy-start.29
  22.6 198.1 %all-reduce.7.cloned.1.call-start = ((), (), s32[]{:S(2)}) async-start(), calls=%async_computation.6 | async-start | bytes 2097152 | tf_op jit(solution)/shard_map/psum | solution.py:68
  161.1 61.7 %all-gather.19.cloned.1.call-start = ((), (), s32[]{:S(2)}) async-start(), calls=%async_computation.17 | async-start | bytes 6303744 | tf_op jit(solution)/shard_map/all_gather | solution.py:58
  161.7 90.7 %all-gather.21.cloned.1.call-start = ((), (), s32[]{:S(2)}) async-start(), calls=%async_computation.18 | async-start | bytes 6303744 | tf_op jit(solution)/shard_map/all_gather | solution.py:63
  162.2 135.4 %all-gather.23.cloned.1.call-start = ((), (), s32[]{:S(2)}) async-start(), calls=%async_computation.19 | async-start | bytes 6303744 | tf_op jit(solution)/shard_map/all_gather | solution.py:67
  162.8 152.3 %reduce-scatter.11.cloned.1.call-start = ((), (), s32[]{:S(2)}) async-start(), calls=%async_computation.9 | async-start | bytes 655360 | tf_op jit(solution)/shard_map/reduce_scatter | solution.py:91
  187.4 3.2 copy-start.26
  190.5 3.2 copy-start.30
  195.2 174.5 %all-reduce.9.cloned.1.call-start = ((), (), s32[]{:S(2)}) async-start(), calls=%async_computation.7 | async-start | bytes 2097152 | tf_op jit(solution)/shard_map/psum | solution.py:68
  228.2 81.3 %copy-start.24 = (s32[2]{0:T(128)S(1)}, s32[2]{0:T(128)}, u32[]{:S(2)}) copy-start(s32[2]{0:T(128)} %param.24) | copy-start | bytes 28
  309.5 104.3 %all-reduce.11.cloned.1.call-start = ((), (), s32[]{:S(2)}) async-start(), calls=%async_computation.10 | async-start | bytes 1048576 | tf_op jit(solution)/shard_map/psum | solution.py:117
  375.7 96.3 %all-reduce.13.cloned.1.call-start = ((), (), s32[]{:S(2)}) async-start(), calls=%async_computation.21 | async-start | bytes 2097152 | tf_op jit(solution)/shard_map/psum | solution.py:141
  413.8 3.6 copy-start.27
  413.8 5.3 copy-start.28
  417.3 3.3 copy-start.17
  420.6 92.7 %reduce-scatter.17.cloned.1.call-start = ((), (), s32[]{:S(2)}) async-start(), calls=%async_computation.13 | async-start | bytes 1179648 | tf_op jit(solution)/shard_map/reduce_scatter | solution.py:162
  423.3 123.2 %reduce-scatter.19.cloned.1.call-start = ((), (), s32[]{:S(2)}) async-start(), calls=%async_computation.20 | async-start | bytes 4718592
  472.0 3.0 copy-start.15
  495.9 105.1 %reduce-scatter.15.cloned.1.call-start = ((), (), s32[]{:S(2)}) async-start(), calls=%async_computation.12 | async-start | bytes 4718592 | tf_op jit(solution)/shard_map/reduce_scatter | solution.py:156
  497.7 3.4 copy-start.35
  504.4 150.9 %reduce-scatter.13.cloned.1.call-start = ((), (), s32[]{:S(2)}) async-start(), calls=%async_computation.11 | async-start | bytes 4718592 | tf_op jit(solution)/shard_map/reduce_scatter | solution.py:153
  548.4 153.5 %copy-start.1 = (bf16[1024,512]{1,0:T(8,128)(2,1)S(1)}, bf16[1024,512]{1,0:T(8,128)(2,1)}, u32[]{:S(2)}) copy-start(bf16[1024,512]{1,0:T(8,128)(2,1)} %param.23) | copy-start | bytes 3145732
  550.2 151.2 %copy-start.31 = (f32[4]{0:T(128)S(1)}, f32[4]{0:T(128)}, u32[]{:S(2)}) copy-start(f32[4]{0:T(128)} %constant.52) | copy-start | bytes 52
  (23 other events, 31.0 us)
Sparse Core Ops, SparseCore 0:
  10.9 46.2 all-gather.12
  59.6 43.5 all-gather.14
  105.7 43.5 all-gather.16
  163.5 43.5 all-gather.18
  208.8 43.5 all-gather.20
  254.1 43.5 all-gather.22
  424.6 35.5 reduce-scatter.16
  496.0 50.4 reduce-scatter.18
  549.8 51.0 reduce-scatter.14
  604.2 51.0 reduce-scatter.12
Sparse Core Ops, SparseCore 1:
  22.6 24.6 reduce-scatter.8
  161.2 59.4 all-reduce.6
  223.4 21.1 reduce-scatter.10
  309.6 60.1 all-reduce.8
  375.8 37.9 all-reduce.10
  420.7 51.3 all-reduce.12
where the time goes:
time: 718 us; the launch traced here: 710 us
  waiting for transfers between devices  460 us (64%)
  blocking collectives  85.4 us (12%)
  matrix products  69.7 us (10%)
  local copies, waits for them, and re-layouts  39.6 us (6%)
  other arithmetic  33.1 us (5%)
  between operations  20.3 us (3%)
    all_gather x2, waiting for transfers between devices, per_device(): down_full = lax.all_gather(t_down[k], 'dp', axis=1, tiled=True)  91.3 us
    all_gather x2, waiting for transfers between devices, per_device(): lax.all_gather(t_up[k], 'dp', axis=0, tiled=True)  64.7 us
    psum x2, waiting for transfers between devices, per_device(): lax.psum(jnp.dot(hidden, down_full, preferred_element_type=jnp.float32).a...  56 us
    reduce_scatter x1, waiting for transfers between devices, per_device(): lax.psum_scatter(jnp.stack(gate_grads).astype(jnp.bfloat16), 'dp', scatte...  51.5 us
    reduce_scatter x1, waiting for transfers between devices, per_device(): lax.psum_scatter(jnp.stack(up_grads).astype(jnp.bfloat16), 'dp', scatter_...  50.8 us
    all_gather x2, blocking collectives, per_device(): states.append(lax.all_gather(own_next, 'tensor', axis=0, tiled=True))  46.1 us
    psum x1, waiting for transfers between devices, per_device(): lax.psum(proj_part.astype(jnp.bfloat16), 'tensor').astype(jnp.float32)  45.5 us
    psum x1, blocking collectives, per_device(): error_total = lax.psum(error_local, ('dp', 'tensor'))  39.2 us
  transfers between devices with their start and end apart: 16, of which 12 were waited for; matrix products, arithmetic and copies ran while one was open for 15% of the time, Pallas kernels for 0%

commit v1 on v0

--- a/solution.py
+++ b/solution.py
@@ -10,6 +10,11 @@
 S_LAYERS = 2
 SEQ = 512
 EPSILON = 1e-05
+
+
+def add_all(x, axis):
+    parts = lax.all_gather(x, axis)
+    return jnp.sum(parts, axis=0)
 
 
 def inverse_rms(values):
@@ -65,7 +70,7 @@
         )
         hidden = (jax.nn.silu(gate_act) * up_act).astype(jnp.bfloat16)
         down_full = lax.all_gather(t_down[k], "dp", axis=1, tiled=True)
-        summed = lax.psum(
+        summed = add_all(
             jnp.dot(hidden, down_full, preferred_element_type=jnp.float32).astype(jnp.bfloat16),
             "tensor",
         ).astype(jnp.float32)

time: 718 us -> 842 us (1.17)
  waiting for transfers between devices: 460 us -> 579 us
  other arithmetic: 33.1 us -> 41.8 us
    all_gather x0 -> x2, waiting for transfers between devices: none -> 112 us  [add_all(): parts = lax.all_gather(x, axis)]
    psum x2 -> x0, waiting for transfers between devices: 56 us -> none  [per_device(): lax.psum(jnp.dot(hidden, down_full, preferred_element_type=jnp.float32).a...]
    all_gather x2, waiting for transfers between devices: 34.2 us -> 72.5 us  [per_device(): lax.all_gather(t_gate[k], 'dp', axis=0, tiled=True)]
    all_gather x2, waiting for transfers between devices: 64.7 us -> 91.4 us  [per_device(): lax.all_gather(t_up[k], 'dp', axis=0, tiled=True)]
    all_gather x2, waiting for transfers between devices: 91.3 us -> 80.4 us  [per_device(): down_full = lax.all_gather(t_down[k], 'dp', axis=1, tiled=True)]
    reduce_sum x0 -> x2, other arithmetic: none -> 8.5 us  [add_all(): return jnp.sum(parts, axis=0)]
  transfers between devices with their start and end apart: 16 -> 16, of which waited for: 12 -> 14; matrix products, arithmetic and copies ran while one was open for 15% -> 14% of each run, Pallas kernels for 0% -> 0%
where the time goes in v1:
time: 842 us; the launch traced here: 834 us
  waiting for transfers between devices  579 us (69%)
  blocking collectives  82.6 us (10%)
  matrix products  69.7 us (8%)
  other arithmetic  41.8 us (5%)
  local copies, waits for them, and re-layouts  39.1 us (5%)
  between operations  20.4 us (2%)
    all_gather x2, waiting for transfers between devices, add_all(): parts = lax.all_gather(x, axis)  112 us
    all_gather x2, waiting for transfers between devices, per_device(): lax.all_gather(t_up[k], 'dp', axis=0, tiled=True)  91.4 us
    all_gather x2, waiting for transfers between devices, per_device(): down_full = lax.all_gather(t_down[k], 'dp', axis=1, tiled=True)  80.4 us
    all_gather x2, waiting for transfers between devices, per_device(): lax.all_gather(t_gate[k], 'dp', axis=0, tiled=True)  72.5 us
    reduce_scatter x1, waiting for transfers between devices, per_device(): lax.psum_scatter(jnp.stack(up_grads).astype(jnp.bfloat16), 'dp', scatter_...  51.7 us
    reduce_scatter x1, waiting for transfers between devices, per_device(): lax.psum_scatter(jnp.stack(gate_grads).astype(jnp.bfloat16), 'dp', scatte...  50.6 us
    psum x1, waiting for transfers between devices, per_device(): lax.psum(proj_part.astype(jnp.bfloat16), 'tensor').astype(jnp.float32)  45.5 us
    all_gather x2, blocking collectives, per_device(): states.append(lax.all_gather(own_next, 'tensor', axis=0, tiled=True))  43.4 us
  transfers between devices with their start and end apart: 16, of which 14 were waited for; matrix products, arithmetic and copies ran while one was open for 14% of the time, Pallas kernels for 0%

profile of v1, /device:TPU:0, one launch (start us, length us, event | category | flops | bytes accessed | tf_op | source)
XLA Modules:
  0.0 833.5 jit_solution(407378749247602792)
XLA Ops:
  8.1 2.7 fusion.110
  12.1 2.5 fusion.111
  23.0 34.2 %all-gather.17.cloned.1.call-done = bf16[1,2048,1368]{1,2,0:T(8,128)(2,1)} async-done(((bf16[1,256,1368]{1,2,0:T(8,128)(2,1)}), bf16[1,2048,1368]{1,2,0:T(8,128)(2,1)}) %all-gather.17.cloned.1.call-update) | async-done | bytes 5603344 | tf_op jit(solution)/shard_map/all_gather | solution.py:63
  57.2 5.5 fusion.10
  62.7 40.5 %all-gather.21.cloned.1.call-done = bf16[1,1368,2048]{2,1,0:T(8,128)(2,1)} async-done(((bf16[1,1368,256]{2,1,0:T(8,128)(2,1)}), bf16[1,1368,2048]{2,1,0:T(8,128)(2,1)}) %all-gather.21.cloned.1.call-update) | async-done | bytes 5603344 | tf_op jit(solution)/shard_map/all_gather | solution.py:72
  103.2 46.0 %all-gather.19.cloned.1.call-done = bf16[1,2048,1368]{1,2,0:T(8,128)(2,1)} async-done(((bf16[1,256,1368]{1,2,0:T(8,128)(2,1)}), bf16[1,2048,1368]{1,2,0:T(8,128)(2,1)}) %all-gather.19.cloned.1.call-update) | async-done | bytes 5603344 | tf_op jit(solution)/shard_map/all_gather | solution.py:68
  149.3 11.8 %fusion.24 = bf16[256,2048]{1,0:T(8,128)(2,1)} fusion(bf16[1,1368,2048]{2,1,0:T(8,128)(2,1)} %all-gather.21.cloned.1.call-done, bf16[1,2048,1368]{1,2,0:T(8,128)(2,1)} %all-gather.19.cloned.1.call-done, f32[256,1368]{0,1:T(8,128)} %fusion.10, bf16[256,2048]{1,0:T(8,128)(2,1)S(1)} %copy-done.3, f32[2048]{0:T(1024)S(1)} %bitcast.156, f32[256]{0:T(256)S(1)} %add_rsqrt_fusion.3), kind=kOutput, calls=%fused_computation.25 | convolution fusion | flops 2873626624 | bytes 14713856 | tf_op jit(solution)/shard_map/dot_general | solution.py:74
  164.3 23.1 %all_gather.46 = bf16[256,1024]{1,0:T(8,128)(2,1)S(1)} all-gather(bf16[64,1024]{1,0:T(8,128)(2,1)S(1)} %add_convert_fusion.3), channel_id=1, replica_groups=mesh['dp'=8,'tensor'=4] {'tensor'}, dimensions={0}, use_global_device_ids=true | all-gather | bytes 655360 | tf_op jit(solution)/shard_map/all_gather | solution.py:104
  195.2 51.6 %all-gather.23.cloned.1.call-done = bf16[1024,2048]{1,0:T(8,128)(2,1)} async-done(((bf16[256,2048]{1,0:T(8,128)(2,1)}), bf16[1024,2048]{1,0:T(8,128)(2,1)}) %all-gather.23.cloned.1.call-update) | async-done | bytes 4194320 | tf_op jit(solution)/shard_map/all_gather | solution.py:16
  246.8 4.2 reduce_sum.124
  253.1 38.3 %all-gather.25.cloned.1.call-done = bf16[1,2048,1368]{1,2,0:T(8,128)(2,1)} async-done(((bf16[1,256,1368]{1,2,0:T(8,128)(2,1)}), bf16[1,2048,1368]{1,2,0:T(8,128)(2,1)}) %all-gather.25.cloned.1.call-update) | async-done | bytes 5603344 | tf_op jit(solution)/shard_map/all_gather | solution.py:63
  291.4 5.5 fusion.4
  296.9 39.8 %all-gather.29.cloned.1.call-done = bf16[1,1368,2048]{2,1,0:T(8,128)(2,1)} async-done(((bf16[1,1368,256]{2,1,0:T(8,128)(2,1)}), bf16[1,1368,2048]{2,1,0:T(8,128)(2,1)}) %all-gather.29.cloned.1.call-update) | async-done | bytes 5603344 | tf_op jit(solution)/shard_map/all_gather | solution.py:72
  336.8 45.3 %all-gather.27.cloned.1.call-done = bf16[1,2048,1368]{1,2,0:T(8,128)(2,1)} async-done(((bf16[1,256,1368]{1,2,0:T(8,128)(2,1)}), bf16[1,2048,1368]{1,2,0:T(8,128)(2,1)}) %all-gather.27.cloned.1.call-update) | async-done | bytes 5603344 | tf_op jit(solution)/shard_map/all_gather | solution.py:68
  382.1 11.8 %fusion.27 = bf16[256,2048]{1,0:T(8,128)(2,1)} fusion(bf16[1,1368,2048]{2,1,0:T(8,128)(2,1)} %all-gather.29.cloned.1.call-done, bf16[1,2048,1368]{1,2,0:T(8,128)(2,1)} %all-gather.27.cloned.1.call-done, f32[256,1368]{0,1:T(8,128)} %fusion.4, bf16[256,2048]{1,0:T(8,128)(2,1)S(1)} %get-tuple-element.20, f32[2048]{0:T(1024)S(1)} %bitcast.154, ...), kind=kOutput, calls=%fused_computation.26 | convolution fusion | flops 2873626624 | bytes 14713856 | tf_op jit(solution)/shard_map/dot_general | solution.py:74
  399.6 7.1 reduce-scatter.11.cloned.1.call-done
  407.8 20.2 %all_gather.47 = bf16[256,1024]{1,0:T(8,128)(2,1)} all-gather(bf16[64,1024]{1,0:T(8,128)(2,1)S(1)} %add_convert_fusion.2), channel_id=1, replica_groups=mesh['dp'=8,'tensor'=4] {'tensor'}, dimensions={0}, use_global_device_ids=true | all-gather | bytes 655360 | tf_op jit(solution)/shard_map/all_gather | solution.py:104
  428.0 60.8 %all-gather.31.cloned.1.call-done = bf16[1024,2048]{1,0:T(8,128)(2,1)} async-done(((bf16[256,2048]{1,0:T(8,128)(2,1)}), bf16[1024,2048]{1,0:T(8,128)(2,1)}) %all-gather.31.cloned.1.call-update) | async-done | bytes 4194320 | tf_op jit(solution)/shard_map/all_gather | solution.py:16
  488.9 4.2 reduce_sum.126
  503.3 34.3 %all-reduce.5.cloned.1.call-done = bf16[256,1024]{1,0:T(8,128)(2,1)} async-done(((bf16[256,1024]{1,0:T(8,128)(2,1)}), bf16[256,1024]{1,0:T(8,128)(2,1)}) %all-reduce.5.cloned.1.call-update) | async-done | bytes 524304 | tf_op jit(solution)/shard_map/psum | solution.py:122
  537.6 3.5 multiply_convert_fusion.2
  547.2 3.1 convert_bitcast_fusion
  550.3 45.5 %all-reduce.7.cloned.1.call-done = (bf16[256,1024]{1,0:T(8,128)(2,1)}, bf16[256,1024]{1,0:T(8,128)(2,1)}) async-done(((bf16[256,1024]{1,0:T(8,128)(2,1)}, bf16[256,1024]{1,0:T(8,128)(2,1)}), (bf16[256,1024]{1,0:T(8,128)(2,1)}, bf16[256,1024]{1,0:T(8,128)(2,1)})) %all-reduce.7.cloned.1.call-update) | async-done | bytes 1048592 | tf_op jit(solution)/shard_map/psum | solution.py:146
  602.8 11.3 %copy.20 = bf16[2,1024,1024]{1,0,2:T(2,128)(2,1)} copy(bf16[2,1024,1024]{2,1,0:T(8,128)(2,1)} %pad_maximum_fusion.2) | data formatting | bytes 8388608
  614.1 5.6 copy.22
  639.2 31.1 %reduce-scatter.19.cloned.1.call-done = bf16[128,2048]{1,0:T(8,128)(2,1)} async-done(((bf16[1024,2048]{1,0:T(8,128)(2,1)}), bf16[128,2048]{1,0:T(8,128)(2,1)}) %reduce-scatter.19.cloned.1.call-update) | async-done | bytes 524304
  674.0 50.6 %reduce-scatter.13.cloned.1.call-done = bf16[2,128,1024]{2,1,0:T(8,128)(2,1)} async-done(((bf16[2,1024,1024]{2,1,0:T(8,128)(2,1)}), bf16[2,128,1024]{2,1,0:T(8,128)(2,1)}) %reduce-scatter.13.cloned.1.call-update) | async-done | bytes 524304 | tf_op jit(solution)/shard_map/reduce_scatter | solution.py:158
  724.6 2.8 multiply_reduce_fusion.2
  727.5 51.7 %reduce-scatter.15.cloned.1.call-done = bf16[2,128,1024]{2,1,0:T(8,128)(2,1)} async-done(((bf16[2,1024,1024]{2,1,0:T(8,128)(2,1)}), bf16[2,128,1024]{2,1,0:T(8,128)(2,1)}) %reduce-scatter.15.cloned.1.call-update) | async-done | bytes 524304 | tf_op jit(solution)/shard_map/reduce_scatter | solution.py:161
  779.1 2.8 multiply_reduce_fusion.1
  782.0 2.6 pad_maximum_fusion.5
  785.4 39.2 %all-reduce = (f32[2]{0:T(128)S(1)}, f32[4]{0:T(128)S(1)}) all-reduce(f32[2]{0:T(128)S(1)} %pad_maximum_fusion.4, f32[4]{0:T(128)S(1)} %pad_maximum_fusion.5), channel_id=1, replica_groups=mesh['dp'=8,'tensor'=4] {'dp','tensor'}, use_global_device_ids=true, to_apply=%region_18.19 | all-reduce | flops 6 | bytes 48 | tf_op jit(solution)/shard_map/psum | solution.py:121
  (167 shorter events, 73.5 us)
Async XLA Ops:
  8.0 487.8 %copy-start = (bf16[1024,512]{1,0:T(8,128)(2,1)S(1)}, bf16[1024,512]{1,0:T(8,128)(2,1)}, u32[]{:S(2)}) copy-start(bf16[1024,512]{1,0:T(8,128)(2,1)} %param.23) | copy-start | bytes 3145732
  8.0 49.2 %all-gather.17.cloned.1.call-start = ((), (), s32[]{:S(2)}) async-start(), calls=%async_computation.12 | async-start | bytes 6303744 | tf_op jit(solution)/shard_map/all_gather | solution.py:63
  10.8 92.4 %all-gather.21.cloned.1.call-start = ((), (), s32[]{:S(2)}) async-start(), calls=%async_computation.14 | async-start | bytes 6303744 | tf_op jit(solution)/shard_map/all_gather | solution.py:72
  12.0 2.9 copy-start.23
  12.0 137.2 %all-gather.19.cloned.1.call-start = ((), (), s32[]{:S(2)}) async-start(), calls=%async_computation.13 | async-start | bytes 6303744 | tf_op jit(solution)/shard_map/all_gather | solution.py:68
  14.7 148.7 %reduce-scatter.9.cloned.1.call-start = ((), (), s32[]{:S(2)}) async-start(), calls=%async_computation.6 | async-start | bytes 655360 | tf_op jit(solution)/shard_map/reduce_scatter | solution.py:96
  17.8 3.3 copy-start.29
  19.6 3.0 copy-start.14
  22.6 224.2 %all-gather.23.cloned.1.call-start = ((), (), s32[]{:S(2)}) async-start(), calls=%async_computation.15 | async-start | bytes 5242880 | tf_op jit(solution)/shard_map/all_gather | solution.py:16
  161.1 130.3 %all-gather.25.cloned.1.call-start = ((), (), s32[]{:S(2)}) async-start(), calls=%async_computation.16 | async-start | bytes 6303744 | tf_op jit(solution)/shard_map/all_gather | solution.py:63
  161.7 175.1 %all-gather.29.cloned.1.call-start = ((), (), s32[]{:S(2)}) async-start(), calls=%async_computation.18 | async-start | bytes 6303744 | tf_op jit(solution)/shard_map/all_gather | solution.py:72
  162.4 219.7 %all-gather.27.cloned.1.call-start = ((), (), s32[]{:S(2)}) async-start(), calls=%async_computation.17 | async-start | bytes 6303744 | tf_op jit(solution)/shard_map/all_gather | solution.py:68
  163.2 243.5 %reduce-scatter.11.cloned.1.call-start = ((), (), s32[]{:S(2)}) async-start(), calls=%async_computation.7 | async-start | bytes 655360 | tf_op jit(solution)/shard_map/reduce_scatter | solution.py:96
  187.6 2.9 copy-start.26
  190.5 3.2 copy-start.30
  192.3 2.8 copy-start.16
  195.2 293.7 %all-gather.31.cloned.1.call-start = ((), (), s32[]{:S(2)}) async-start(), calls=%async_computation.19 | async-start | bytes 5242880 | tf_op jit(solution)/shard_map/all_gather | solution.py:16
  296.9 97.1 %copy-start.24 = (s32[2]{0:T(128)S(1)}, s32[2]{0:T(128)}, u32[]{:S(2)}) copy-start(s32[2]{0:T(128)} %param.24) | copy-start | bytes 28
  394.0 143.6 %all-reduce.5.cloned.1.call-start = ((), (), s32[]{:S(2)}) async-start(), calls=%async_computation.8 | async-start | bytes 1048576 | tf_op jit(solution)/shard_map/psum | solution.py:122
  499.0 96.8 %all-reduce.7.cloned.1.call-start = ((), (), s32[]{:S(2)}) async-start(), calls=%async_computation.21 | async-start | bytes 2097152 | tf_op jit(solution)/shard_map/psum | solution.py:146
  537.6 3.6 copy-start.27
  537.6 5.3 copy-start.28
  541.1 3.3 copy-start.19
  544.4 92.5 %reduce-scatter.17.cloned.1.call-start = ((), (), s32[]{:S(2)}) async-start(), calls=%async_computation.11 | async-start | bytes 1179648 | tf_op jit(solution)/shard_map/reduce_scatter | solution.py:167
  547.1 123.2 %reduce-scatter.19.cloned.1.call-start = ((), (), s32[]{:S(2)}) async-start(), calls=%async_computation.20 | async-start | bytes 4718592
  595.8 3.0 copy-start.15
  619.7 104.9 %reduce-scatter.13.cloned.1.call-start = ((), (), s32[]{:S(2)}) async-start(), calls=%async_computation.9 | async-start | bytes 4718592 | tf_op jit(solution)/shard_map/reduce_scatter | solution.py:158
  621.5 3.5 copy-start.35
  621.6 3.5 copy-start.38
  628.5 150.7 %reduce-scatter.15.cloned.1.call-start = ((), (), s32[]{:S(2)}) async-start(), calls=%async_computation.10 | async-start | bytes 4718592 | tf_op jit(solution)/shard_map/reduce_scatter | solution.py:161
  672.3 153.4 %copy-start.1 = (bf16[1024,512]{1,0:T(8,128)(2,1)S(1)}, bf16[1024,512]{1,0:T(8,128)(2,1)}, u32[]{:S(2)}) copy-start(bf16[1024,512]{1,0:T(8,128)(2,1)} %param.23) | copy-start | bytes 3145732
  674.0 151.1 %copy-start.31 = (f32[4]{0:T(128)S(1)}, f32[4]{0:T(128)}, u32[]{:S(2)}) copy-start(f32[4]{0:T(128)} %constant.55) | copy-start | bytes 52
  (23 other events, 35.6 us)
Sparse Core Ops, SparseCore 0:
  10.9 46.2 all-gather.16
  59.6 43.5 all-gather.20
  105.7 43.5 all-gather.18
  548.1 35.5 reduce-scatter.16
  619.8 50.4 reduce-scatter.18
  673.5 51.0 reduce-scatter.12
  728.0 51.0 reduce-scatter.14
Sparse Core Ops, SparseCore 1:
  22.7 24.6 reduce-scatter.8
  161.2 85.6 all-gather.22
  248.6 42.8 all-gather.24
  293.3 43.4 all-gather.28
  338.7 43.4 all-gather.26
  385.0 21.7 reduce-scatter.10
  408.7 80.1 all-gather.30
  499.1 38.4 all-reduce.4
  544.5 51.3 all-reduce.6
